TPU v7x, 1024 devices: a whole 8x8x8 slice. The times are simulated.
1024 devices in a mesh: prow: 16 (over y, core), pcol: 64 (over x, z).
Axes of the slice: x: 8, y: 8, z: 8, core: 2. Of those that a mesh axis runs over, the one named last changes fastest.
Arguments:
- slab: bfloat16 [32768, 24576], P('prow', 'pcol'), may hold values from -6 to 6
- pivots: int32 [512], replicated, may hold values from 0 to 32767, as said below
- l_top: bfloat16 [512, 512], replicated, may hold values from -0.125 to 0.125
- l_panel_t: bfloat16 [512, 32768], P('pcol', 'prow'), may hold values from -0.125 to 0.125
Outputs:
- result: bfloat16 [32768, 24576], P('prow', 'pcol')
Inputs may be any that keep to these rules, and one draw needn't show every extreme that they name: `pivots`: distinct rows; how many fall on each index of prow is uneven and changes with the draw.
All inputs are finite; a program needn't handle non-finite values.
Results may differ from a plain program's by a relative error of at most 0.0029.
Values may be sent and summed in bfloat16 or wider, within the bound.
No kernel may reach another device: no remote copies, remote signals or barrier semaphores. Data moves between devices by JAX's collectives and lax.ppermute only.
A program may use at most 64 MiB of HBM per device.

v0:
```python
import jax
import jax.numpy as jnp
from jax import lax
from jax.experimental import pallas as pl
from jax.experimental.pallas import tpu as pltpu
from jax.sharding import PartitionSpec as P


BF, F32 = jnp.bfloat16, jnp.float32
HI = lax.Precision.HIGHEST


CAP = 80
ROOM = pltpu.CompilerParams(vmem_limit_bytes=20 * 2**20)


def column(row):
    n = row.shape[1]
    eye = lax.broadcasted_iota(jnp.int32, (n, n), 0) == lax.broadcasted_iota(jnp.int32, (n, n), 1)
    return jnp.sum(jnp.where(eye, row, 0.0), axis=1, keepdims=True)


def pick_kernel(where_ref, pivot_ref, slab_ref, pick_ref, place_ref, dest_ref, most_ref):
    n, rows = pivot_ref.shape[1], slab_ref.shape[0]
    me, base = where_ref[0], where_ref[1].astype(F32)
    p_int = pivot_ref[...]
    p_row = p_int.astype(F32)
    p_col = column(p_row)
    o_row = (p_int // rows).astype(F32)
    o_col = column(o_row)
    sub = lax.broadcasted_iota(jnp.int32, (n, n), 0)
    lane = lax.broadcasted_iota(jnp.int32, (n, n), 1)
    same = o_col == o_row
    rank_row = jnp.sum(jnp.where(same & (sub < lane), 1.0, 0.0), axis=0, keepdims=True)
    rank_col = jnp.sum(jnp.where(same & (lane < sub), 1.0, 0.0), axis=1, keepdims=True)
    most_ref[0] = jnp.max(rank_row).astype(jnp.int32) + 1
    slot = rank_col - base
    place_ref[...] = jnp.where((slot >= 0) & (slot < CAP), o_col * CAP + slot, -1.0).astype(jnp.int32)

    index = lax.broadcasted_iota(jnp.int32, (CAP, n), 0).astype(F32) + base
    chosen = (o_row == me.astype(F32)) & (rank_row == index)
    local = jnp.sum(jnp.where(chosen, p_row - (me * rows).astype(F32), 0.0), axis=1, keepdims=True)
    hot = lax.broadcasted_iota(jnp.int32, (CAP, rows), 1) == local.astype(jnp.int32)
    pick_ref[...] = jnp.dot(hot.astype(BF), slab_ref[...], preferred_element_type=F32).astype(BF)

    taken = jnp.where(p_col == lane.astype(F32), 1.0, 0.0)
    free_row = 1.0 - jnp.max(taken, axis=0, keepdims=True)
    free_col = column(free_row)
    far_row = jnp.where(p_row >= n, 1.0, 0.0)
    far_col = jnp.where(p_col >= n, 1.0, 0.0)
    free_rank = jnp.sum(jnp.where(sub < lane, free_col, 0.0), axis=0, keepdims=True)
    far_rank = jnp.sum(jnp.where(lane < sub, far_row, 0.0), axis=1, keepdims=True)
    match = (far_rank == free_rank) & (far_col > 0) & (free_row > 0)
    dest_ref[...] = (jnp.sum(jnp.where(match, p_col + 1.0, 0.0), axis=0, keepdims=True) - 1.0).astype(jnp.int32)


def pick(where, pivots, slab):
    n, w = pivots.shape[0], slab.shape[1]
    vmem = pl.BlockSpec(memory_space=pltpu.VMEM)
    return pl.pallas_call(
        pick_kernel,
        in_specs=[pl.BlockSpec(memory_space=pltpu.SMEM), vmem, vmem],
        out_shape=[
            jax.ShapeDtypeStruct((CAP, w), BF),
            jax.ShapeDtypeStruct((n, 1), jnp.int32),
            jax.ShapeDtypeStruct((1, n), jnp.int32),
            jax.ShapeDtypeStruct((1,), jnp.int32),
        ],
        out_specs=[vmem, vmem, vmem, pl.BlockSpec(memory_space=pltpu.SMEM)],
        compiler_params=ROOM,
        cost_estimate=pl.CostEstimate(flops=2 * 10**9, bytes_accessed=2 * slab.size, transcendentals=0),
    )(where, pivots[None], slab)


def mm(a, b):
    return jnp.dot(a, b, precision=HI, preferred_element_type=F32)


def inverse_kernel(l_ref, a_ref, b_ref, x_ref):
    n, t = l_ref.shape[0], 128
    row = lax.broadcasted_iota(jnp.int32, (t, t), 0)
    col = lax.broadcasted_iota(jnp.int32, (t, t), 1)
    eye = (row == col).astype(F32)
    x_ref[...] = jnp.zeros_like(x_ref)
    blocks = range(n // t)
    low = [
        jnp.where(row > col, l_ref[b * t : (b + 1) * t, b * t : (b + 1) * t].astype(F32), 0.0)
        for b in blocks
    ]
    step = 16
    near = [jnp.where(row // step == col // step, v, 0.0) for v in low]
    inv = [eye - v for v in near]
    power = near
    for _ in range(3):
        power = [mm(v, v) for v in power]
        inv = [x + mm(x, v) for x, v in zip(inv, power)]
    while step < t:
        off = [
            jnp.where((row // (2 * step) == col // (2 * step)) & (row // step != col // step), v, 0.0)
            for v in low
        ]
        half = [mm(x, v) for x, v in zip(inv, off)]
        inv = [x - mm(h, x) for x, h in zip(inv, half)]
        step *= 2
    for b in blocks:
        x_ref[b * t : (b + 1) * t, b * t : (b + 1) * t] = inv[b]
    size = t
    while size < n:
        for s in range(0, n, 2 * size):
            top, bot = slice(s, s + size), slice(s + size, s + 2 * size)
            x_ref[bot, top] = -mm(x_ref[bot, bot], mm(l_ref[bot, top].astype(F32), x_ref[top, top]))
        size *= 2
    x = x_ref[...]
    a = x.astype(BF)
    a_ref[...] = a
    b_ref[...] = (x - a.astype(F32)).astype(BF)


def inverse(l_top):
    n = l_top.shape[0]
    shape = jax.ShapeDtypeStruct((n, n), BF)
    return pl.pallas_call(
        inverse_kernel,
        out_shape=[shape] * 2,
        scratch_shapes=[pltpu.VMEM((n, n), F32)],
        compiler_params=ROOM,
        cost_estimate=pl.CostEstimate(flops=2 * 10**9, bytes_accessed=4 * n * n * 2, transcendentals=0),
    )(l_top)


def placed(place_ref, got_ref):
    hot = lax.broadcasted_iota(jnp.int32, (place_ref.shape[0], got_ref.shape[0]), 1) == place_ref[...]
    return jnp.dot(hot.astype(BF), got_ref[...], preferred_element_type=F32)


def finish(row_ref, a_ref, b_ref, top, u_ref, v_ref):
    u = jnp.dot(b_ref[...], top, preferred_element_type=F32)
    u += jnp.dot(a_ref[...], top, preferred_element_type=F32)
    u_ref[...] = u.astype(BF)
    v_ref[...] = (-u).astype(BF)

    @pl.when(row_ref[0] % 2 == 1)
    def _():
        v = [u[(8 * x + z) * 8 : (8 * x + z + 1) * 8] for z in range(8) for x in range(8)]
        v_ref[...] = (-jnp.concatenate(v, axis=0)).astype(BF)


def place_solve_kernel(row_ref, a_ref, b_ref, place_ref, got_ref, u_ref, v_ref):
    finish(row_ref, a_ref, b_ref, placed(place_ref, got_ref).astype(BF), u_ref, v_ref)


def solve_kernel(row_ref, a_ref, b_ref, top_ref, u_ref, v_ref):
    finish(row_ref, a_ref, b_ref, top_ref[...], u_ref, v_ref)


def add_kernel(top_ref, place_ref, got_ref, out_ref):
    out_ref[...] = (top_ref[...].astype(F32) + placed(place_ref, got_ref)).astype(BF)


def solve(kernel, row, parts, *rest):
    n, w = parts[0].shape[0], rest[-1].shape[1]
    shape = jax.ShapeDtypeStruct((n, w), BF)
    vmem = pl.BlockSpec(memory_space=pltpu.VMEM)
    return tuple(pl.pallas_call(
        kernel,
        in_specs=[pl.BlockSpec(memory_space=pltpu.SMEM)] + [vmem] * (2 + len(rest)),
        out_shape=[shape] * 2,
        compiler_params=ROOM,
        cost_estimate=pl.CostEstimate(flops=10**9, bytes_accessed=10**7, transcendentals=0),
    )(row, *parts, *rest))


def update_kernel(row_ref, l_ref, u_ref, v_ref, dest_ref, own_ref, sent_ref, slab_ref, out_ref, right_ref):
    j = pl.program_id(0)
    rows, w = slab_ref.shape
    n = u_ref.shape[0]

    @pl.when(j == 0)
    def _():
        right_ref[:n, :w] = v_ref[...]
        right_ref[:n, w:] = jnp.zeros_like(right_ref[:n, w:])
        right_ref[n:, w:] = jnp.ones_like(right_ref[n:, w:])

        @pl.when(row_ref[0] % 2 == 0)
        def _():
            right_ref[n:, :w] = own_ref[...]

        @pl.when(row_ref[0] % 2 == 1)
        def _():
            right_ref[n:, :w] = sent_ref[...]

    first = (row_ref[0] * pl.num_programs(0) + j) * rows
    hit = first + lax.broadcasted_iota(jnp.int32, (rows, n), 0) == dest_ref[...]
    left = jnp.concatenate([l_ref[...].T, hit.astype(BF)], axis=1)
    acc = jnp.dot(left, right_ref[...], preferred_element_type=F32)
    lost = jnp.concatenate([acc[:, w:]] * (w // 128), axis=1)
    out_ref[...] = (jnp.where(lost > 0, 0.0, slab_ref[...].astype(F32)) + acc[:, :w]).astype(BF)

    @pl.when((row_ref[0] == 0) & (j * rows < n))
    def _():
        out_ref[...] = u_ref[pl.ds(pl.multiple_of(jnp.minimum(j * rows, n - rows), rows), rows), :]


def update(row, panel, u, v, dest, own, sent, slab, rows):
    n, height = panel.shape
    w = slab.shape[1]
    whole = lambda a: pl.BlockSpec(a.shape, lambda j: (0,) * a.ndim)
    return pl.pallas_call(
        update_kernel,
        grid=(height // rows,),
        in_specs=[
            pl.BlockSpec(memory_space=pltpu.SMEM),
            pl.BlockSpec((n, rows), lambda j: (0, j)),
            *map(whole, (u, v, dest, own, sent)),
            pl.BlockSpec((rows, w), lambda j: (j, 0)),
        ],
        out_specs=pl.BlockSpec((rows, w), lambda j: (j, 0)),
        out_shape=jax.ShapeDtypeStruct(slab.shape, BF),
        scratch_shapes=[pltpu.VMEM((2 * n, w + 128), BF)],
        compiler_params=ROOM,
        cost_estimate=pl.CostEstimate(
            flops=4 * height * n * w, bytes_accessed=2 * n * height + 4 * height * w, transcendentals=0
        ),
    )(row, panel, u, v, dest, own, sent, slab)


def lines(first):
    groups = []
    for row in range(16):
        for i in range(8):
            line = [i * 8 + j if row % 2 == first else j * 8 + i for j in range(8)]
            groups.append([row * 64 + c for c in line])
    return groups


def exchange(block, groups):
    copies = jnp.broadcast_to(block[None], (8,) + block.shape)
    return lax.all_to_all(copies, ("prow", "pcol"), 0, 0, axis_index_groups=groups)


def hand_on(home, size):
    return lax.ppermute(home, "prow", [(i, i + size // 2) for i in range(0, 16, size)])


def step_of_panel(slab, pivots, l_top, l_panel_t):
    local_rows, w = slab.shape
    n = pivots.shape[0]
    k = l_panel_t.shape[0]
    row = lax.axis_index("prow").astype(jnp.int32)
    r = row.reshape(1)

    def picks(base):
        return pick(jnp.stack([row, base]), pivots, slab)

    near = exchange(l_panel_t, lines(0)).reshape(8 * k, local_rows)
    home = slab[:n]
    got = hand_on(home, 16)
    parts = inverse(l_top)
    got, parts = lax.optimization_barrier((got, parts))
    home = jnp.where(row == 0, home, got)
    got = hand_on(home, 8)
    picked, place, dest, most = picks(jnp.int32(0))
    near, got, picked = lax.optimization_barrier((near, got, picked))
    home = jnp.where(row % 8 == 0, home, got)
    got = hand_on(home, 4)
    panel = exchange(near, lines(1)).reshape(n, local_rows)
    got, picked = lax.optimization_barrier((got, picked))
    home = jnp.where(row % 4 == 0, home, got)
    sent = hand_on(home, 2)
    got = lax.all_gather(picked, "prow", axis=0, tiled=True)

    def direct():
        return solve(place_solve_kernel, r, parts, place, got)

    def in_rounds():
        def step(state):
            base, top = state
            picked, place, _, _ = picks(base)
            got = lax.all_gather(picked, "prow", axis=0, tiled=True)
            top = pl.pallas_call(add_kernel, out_shape=jax.ShapeDtypeStruct((n, w), BF))(top, place, got)
            return base + CAP, top

        _, top = lax.while_loop(lambda s: s[0] < most[0], step, (jnp.int32(0), jnp.zeros((n, w), BF)))
        return solve(solve_kernel, r, parts, top)

    u, v = lax.cond(most[0] <= CAP, direct, in_rounds)
    return update(r, panel, u, v, dest, home, sent, slab, 256)


def solution(mesh):
    return jax.shard_map(
        step_of_panel,
        mesh=mesh,
        in_specs=(P("prow", "pcol"), P(), P(), P("pcol", "prow")),
        out_specs=P("prow", "pcol"),
        check_vma=False,
    )
```

profile of v0, /device:TPU:1, one launch (start us, length us, event | category | flops | bytes accessed | tf_op | source)
XLA Modules:
  0.0 90.3 jit_solution(9627984686813291477)
XLA Ops:
  0.0 0.0 copy-start.1
  0.0 1.1 %slice.3 = bf16[512,384]{1,0:T(8,128)(2,1)S(1)} slice(bf16[2048,384]{1,0:T(8,128)(2,1)} %slab_ref.3), slice={[0:512], [0:384]} | slice | bytes 786432 | tf_op jit(solution)/shard_map/slice | solution.py:256
  1.1 0.7 collective-permute-start
  1.8 1.5 %broadcast_in_dim.8 = bf16[8,8,2048]{2,1,0:T(8,128)(2,1)} broadcast(bf16[8,2048]{1,0:T(8,128)(2,1)} %param.11), dimensions={1,2} | broadcast | bytes 294912 | tf_op jit(solution)/shard_map/broadcast_in_dim | solution.py:237
  3.3 7.3 %all-to-all-start = ((bf16[8,8,2048]{2,1,0:T(8,128)(2,1)}), bf16[8,8,2048]{2,1,0:T(8,128)(2,1)S(1)}, u32[]{:S(2)}, u32[]{:S(2)}) async-start(bf16[8,8,2048]{2,1,0:T(8,128)(2,1)} %broadcast_in_dim.8), calls=%async_computation | async-start | bytes 524288 | tf_op jit(solution)/shard_map/all_to_all | solution.py:238
  10.6 0.0 copy-done.1
  10.6 0.0 copy-start.2
  10.6 0.0 copy-start.3
  10.6 5.3 %shard_map.46 = (bf16[512,512]{1,0:T(8,128)(2,1)}, bf16[512,512]{1,0:T(8,128)(2,1)}) custom-call(bf16[512,512]{1,0:T(8,128)(2,1)S(1)} %copy-done.1), custom_call_target="tpu_custom_call" | custom-call | flops 2000000000 | bytes 2097152 | tf_op jit(solution)/shard_map/pallas_call | solution.py:122
  15.9 0.0 collective-permute-done
  15.9 0.0 copy-done.2
  15.9 0.1 broadcast_select_fusion.2
  16.0 0.7 collective-permute-start.1
  16.7 0.1 pad_add_fusion.1.where_ref
  16.7 0.0 copy-done.3
  16.7 2.2 %shard_map.47 = (bf16[80,384]{1,0:T(8,128)(2,1)S(1)}, s32[512,1]{1,0:T(8,128)}, s32[1,512]{1,0:T(1,128)S(1)}, s32[1]{0:T(128)}) custom-call(s32[2]{0:T(128)S(1)} %pad_add_fusion.1.where_ref, s32[1,512]{1,0:T(1,128)S(1)} %bitcast.18, bf16[2048,384]{1,0:T(8,128)(2,1)S(1)} %copy-done.2), custom_call_target="tpu_custom_call" | custom-call | flops 2000000000 | bytes 1572864 | tf_op jit(solution)/shard_map/pallas_call | solution.py:60
  18.9 1.0 %all-to-all-done = bf16[8,8,2048]{2,1,0:T(8,128)(2,1)S(1)} async-done(((bf16[8,8,2048]{2,1,0:T(8,128)(2,1)}), bf16[8,8,2048]{2,1,0:T(8,128)(2,1)S(1)}, u32[]{:S(2)}, u32[]{:S(2)}) %all-to-all-start) | async-done | bytes 262176 | tf_op jit(solution)/shard_map/all_to_all | solution.py:238
  19.9 0.0 collective-permute-done.1
  19.9 1.6 %broadcast_in_dim.20 = bf16[8,64,2048]{2,1,0:T(8,128)(2,1)} broadcast(bf16[64,2048]{1,0:T(8,128)(2,1)S(1)} %bitcast.17), dimensions={1,2} | broadcast | bytes 2359296 | tf_op jit(solution)/shard_map/broadcast_in_dim | solution.py:237
  21.5 16.4 %all-to-all-start.1 = ((bf16[8,64,2048]{2,1,0:T(8,128)(2,1)}), bf16[8,64,2048]{2,1,0:T(8,128)(2,1)S(1)}, u32[]{:S(2)}, u32[]{:S(2)}) async-start(bf16[8,64,2048]{2,1,0:T(8,128)(2,1)} %broadcast_in_dim.20), calls=%async_computation.1 | async-start | bytes 4194304 | tf_op jit(solution)/shard_map/all_to_all | solution.py:238
  38.0 0.7 collective-permute-start.2
  39.3 0.0 collective-permute-done.2
  39.3 0.1 broadcast_select_fusion.own_ref
  39.4 1.3 %collective-permute-start.3 = (bf16[512,384]{1,0:T(8,128)(2,1)S(1)}, bf16[512,384]{1,0:T(8,128)(2,1)S(1)}, u32[]{:S(2)}, u32[]{:S(2)}) collective-permute-start(bf16[512,384]{1,0:T(8,128)(2,1)S(1)} %broadcast_select_fusion.own_ref), channel_id=1, source_target_pairs={{0,64},{128,192},{256,320},{384,448},{512,576},{640,704},{768,832}... | collective-permute-start | bytes 1179656 | tf_op jit(solution)/shard_map/ppermute | solution.py:242
  40.7 37.9 %all_gather.6 = bf16[1280,384]{1,0:T(8,128)(2,1)} all-gather(bf16[80,384]{1,0:T(8,128)(2,1)S(1)} %get-tuple-element.103), channel_id=1, replica_groups=mesh['prow'=16,'pcol'=64] {'prow'}, dimensions={0}, use_global_device_ids=true | all-gather | bytes 1044480 | tf_op jit(solution)/shard_map/all_gather | solution.py:270
  78.6 4.0 %conditional.1 = ((bf16[512,384]{1,0:T(8,128)(2,1)}, bf16[512,384]{1,0:T(8,128)(2,1)})) conditional(s32[]{:T(128)} %bitcast.8, (s32[1]{0:T(128)}, s32[]{:T(128)}, s32[512]{0:T(512)S(1)}, bf16[2048,384]{1,0:T(8,128)(2,1)}, s32[1]{0:T(128)}, /*index=5*/bf16[512,512]{1,0:T(8,128)(2,1)}, bf16[512,512]{1,0:T(8,128)(2,1)}) %tuple.38, (s32[1]{0:T(128)}, ...), branch_computations={%region_0.3_spmd, %region_3.4_spmd} | conditional | flops 3000000000 | bytes 13805387 | solution.py:286
  78.6 4.0 %branch_1_fun.1 = (bf16[512,384]{1,0:T(8,128)(2,1)}, bf16[512,384]{1,0:T(8,128)(2,1)}) custom-call(s32[1]{0:T(128)} %get-tuple-element.71.row_ref, bf16[512,512]{1,0:T(8,128)(2,1)} %get-tuple-element.72.a_ref, bf16[512,512]{1,0:T(8,128)(2,1)} %get-tuple-element.73.b_ref, s32[512,1]{1,0:T(8,128)} %get-tuple-element.74.place_ref, ...), custom_call_target="tpu_custom_call" | custom-call | flops 1000000000 | bytes 10000000 | tf_op jit(solution)/shard_map/cond/branch_1_fun/pallas_call | solution.py:164
  82.6 0.0 collective-permute-done.3.sent_ref
  82.6 0.0 all-to-all-done.1
  82.6 7.6 %shard_map.48 = bf16[2048,384]{1,0:T(8,128)(2,1)} custom-call(s32[1]{0:T(128)} %bitcast.4.row_ref, bf16[512,2048]{1,0:T(8,128)(2,1)S(1)} %bitcast.16, bf16[512,384]{1,0:T(8,128)(2,1)} %get-tuple-element.104.u_ref, bf16[512,384]{1,0:T(8,128)(2,1)} %get-tuple-element.105.v_ref, s32[1,512]{1,0:T(1,128)S(1)} %get-tuple-element.106.dest_ref, ...), custom_call_target="tpu_custom_call" | custom-call | flops 1610612736 | bytes 5242880 | tf_op jit(solution)/shard_map/pallas_call | solution.py:208
  (1 shorter events, 0.0 us)
Async XLA Ops:
  0.0 10.6 %copy-start.1 = (bf16[512,512]{1,0:T(8,128)(2,1)S(1)}, bf16[512,512]{1,0:T(8,128)(2,1)}, u32[]{:S(2)}) copy-start(bf16[512,512]{1,0:T(8,128)(2,1)} %l_ref.1) | copy-start | bytes 1572868
  1.1 14.8 %collective-permute-start = (bf16[512,384]{1,0:T(8,128)(2,1)S(1)}, bf16[512,384]{1,0:T(8,128)(2,1)S(1)}, u32[]{:S(2)}, u32[]{:S(2)}) collective-permute-start(bf16[512,384]{1,0:T(8,128)(2,1)S(1)} %slice.3), channel_id=1, source_target_pairs={{0,512},{1,513},{2,514},{3,515},{4,516},{5,517},{6,518},{7,519},{8... | collective-permute-start | bytes 1179656 | tf_op jit(solution)/shard_map/ppermute | solution.py:242
  3.3 16.6 %all-to-all-start = ((bf16[8,8,2048]{2,1,0:T(8,128)(2,1)}), bf16[8,8,2048]{2,1,0:T(8,128)(2,1)S(1)}, u32[]{:S(2)}, u32[]{:S(2)}) async-start(bf16[8,8,2048]{2,1,0:T(8,128)(2,1)} %broadcast_in_dim.8), calls=%async_computation | async-start | bytes 524288 | tf_op jit(solution)/shard_map/all_to_all | solution.py:238
  10.6 5.3 %copy-start.2 = (bf16[2048,384]{1,0:T(8,128)(2,1)S(1)}, bf16[2048,384]{1,0:T(8,128)(2,1)}, u32[]{:S(2)}) copy-start(bf16[2048,384]{1,0:T(8,128)(2,1)} %slab_ref.3) | copy-start | bytes 4718596
  10.6 6.1 %copy-start.3 = (s32[512]{0:T(512)S(1)}, s32[512]{0:T(512)}, u32[]{:S(2)}) copy-start(s32[512]{0:T(512)} %param.9) | copy-start | bytes 6148
  16.0 3.9 %collective-permute-start.1 = (bf16[512,384]{1,0:T(8,128)(2,1)S(1)}, bf16[512,384]{1,0:T(8,128)(2,1)S(1)}, u32[]{:S(2)}, u32[]{:S(2)}) collective-permute-start(bf16[512,384]{1,0:T(8,128)(2,1)S(1)} %broadcast_select_fusion.2), channel_id=1, source_target_pairs={{0,256},{512,768},{1,257},{513,769},{2,258},{514,770},{3,259},{515... | collective-permute-start | bytes 1179656 | tf_op jit(solution)/shard_map/ppermute | solution.py:242
  21.5 61.1 %all-to-all-start.1 = ((bf16[8,64,2048]{2,1,0:T(8,128)(2,1)}), bf16[8,64,2048]{2,1,0:T(8,128)(2,1)S(1)}, u32[]{:S(2)}, u32[]{:S(2)}) async-start(bf16[8,64,2048]{2,1,0:T(8,128)(2,1)} %broadcast_in_dim.20), calls=%async_computation.1 | async-start | bytes 4194304 | tf_op jit(solution)/shard_map/all_to_all | solution.py:238
  38.0 1.3 %collective-permute-start.2 = (bf16[512,384]{1,0:T(8,128)(2,1)S(1)}, bf16[512,384]{1,0:T(8,128)(2,1)S(1)}, u32[]{:S(2)}, u32[]{:S(2)}) collective-permute-start(bf16[512,384]{1,0:T(8,128)(2,1)S(1)} %broadcast_select_fusion.1), channel_id=1, source_target_pairs={{0,128},{256,384},{512,640},{768,896},{1,129},{257,385},{513,641},... | collective-permute-start | bytes 1179656 | tf_op jit(solution)/shard_map/ppermute | solution.py:242
  39.4 43.2 %collective-permute-start.3 = (bf16[512,384]{1,0:T(8,128)(2,1)S(1)}, bf16[512,384]{1,0:T(8,128)(2,1)S(1)}, u32[]{:S(2)}, u32[]{:S(2)}) collective-permute-start(bf16[512,384]{1,0:T(8,128)(2,1)S(1)} %broadcast_select_fusion.own_ref), channel_id=1, source_target_pairs={{0,64},{128,192},{256,320},{384,448},{512,576},{640,704},{768,832}... | collective-permute-start | bytes 1179656 | tf_op jit(solution)/shard_map/ppermute | solution.py:242
where the time goes:
time: 90.9 us; the launch traced here: 90.3 us
  blocking collectives  37.9 us (42%)
  starting transfers between devices  27.1 us (30%)
  Pallas kernels  19.1 us (21%)
  local copies, waits for them, and re-layouts  4.19 us (5%)
  waiting for transfers between devices  1 us (1%)
    all_gather x1, blocking collectives, step_of_panel(): got = lax.all_gather(picked, 'prow', axis=0, tiled=True)  37.9 us
    all_to_all x2, starting transfers between devices, exchange(): lax.all_to_all(copies, ('prow', 'pcol'), 0, 0, axis_index_groups=groups)  23.7 us
    pallas_call x1, Pallas kernels, update(): pl.pallas_call(update_kernel, grid=(height // rows,), in_specs=[pl.BlockS...  7.65 us
    pallas_call x1, Pallas kernels, inverse(): pl.pallas_call(inverse_kernel, out_shape=[shape] * 2, scratch_shapes=[plt...  5.29 us
    pallas_call x1, Pallas kernels, solve(): pl.pallas_call(kernel, in_specs=[pl.BlockSpec(memory_space=pltpu.SMEM)] +...  4.04 us
    ppermute x4, starting transfers between devices, hand_on(): lax.ppermute(home, 'prow', [(i, i + size // 2) for i in range(0, 16, size)])  3.35 us
    broadcast_in_dim x2, local copies, waits for them, and re-layouts, exchange(): copies = jnp.broadcast_to(block[None], (8,) + block.shape)  3.08 us
    pallas_call x1, Pallas kernels, pick(): pl.pallas_call(pick_kernel, in_specs=[pl.BlockSpec(memory_space=pltpu.SME...  2.17 us
  transfers between devices with their start and end apart: 6, of which 1 were waited for; matrix products, arithmetic and copies ran while one was open for 2% of the time, Pallas kernels for 13%

commit v1 on v0

--- a/solution.py
+++ b/solution.py
@@ -170,58 +170,62 @@
     )(row, *parts, *rest))
 
 
-def update_kernel(row_ref, l_ref, u_ref, v_ref, dest_ref, own_ref, sent_ref, slab_ref, out_ref, right_ref):
+def swap_kernel(row_ref, dest_ref, own_ref, sent_ref, slab_ref, out_ref, right_ref):
     j = pl.program_id(0)
     rows, w = slab_ref.shape
-    n = u_ref.shape[0]
+    n = own_ref.shape[0]
 
     @pl.when(j == 0)
     def _():
-        right_ref[:n, :w] = v_ref[...]
-        right_ref[:n, w:] = jnp.zeros_like(right_ref[:n, w:])
-        right_ref[n:, w:] = jnp.ones_like(right_ref[n:, w:])
+        right_ref[:, w:] = jnp.ones_like(right_ref[:, w:])
 
         @pl.when(row_ref[0] % 2 == 0)
         def _():
-            right_ref[n:, :w] = own_ref[...]
+            right_ref[:, :w] = own_ref[...]
 
         @pl.when(row_ref[0] % 2 == 1)
         def _():
-            right_ref[n:, :w] = sent_ref[...]
+            right_ref[:, :w] = sent_ref[...]
 
     first = (row_ref[0] * pl.num_programs(0) + j) * rows
     hit = first + lax.broadcasted_iota(jnp.int32, (rows, n), 0) == dest_ref[...]
-    left = jnp.concatenate([l_ref[...].T, hit.astype(BF)], axis=1)
-    acc = jnp.dot(left, right_ref[...], preferred_element_type=F32)
+    acc = jnp.dot(hit.astype(BF), right_ref[...], preferred_element_type=F32)
     lost = jnp.concatenate([acc[:, w:]] * (w // 128), axis=1)
-    out_ref[...] = (jnp.where(lost > 0, 0.0, slab_ref[...].astype(F32)) + acc[:, :w]).astype(BF)
+    out_ref[...] = jnp.where(lost > 0, acc[:, :w].astype(BF), slab_ref[...])
+
+
+def update_kernel(row_ref, l_ref, u_ref, v_ref, slab_ref, out_ref):
+    j = pl.program_id(0)
+    rows, n = slab_ref.shape[0], u_ref.shape[0]
+    acc = jnp.dot(l_ref[...].T, v_ref[...], preferred_element_type=F32)
+    out_ref[...] = (slab_ref[...].astype(F32) + acc).astype(BF)
 
     @pl.when((row_ref[0] == 0) & (j * rows < n))
     def _():
         out_ref[...] = u_ref[pl.ds(pl.multiple_of(jnp.minimum(j * rows, n - rows), rows), rows), :]
 
 
-def update(row, panel, u, v, dest, own, sent, slab, rows):
-    n, height = panel.shape
-    w = slab.shape[1]
-    whole = lambda a: pl.BlockSpec(a.shape, lambda j: (0,) * a.ndim)
+def by_rows(kernel, rows, out, args, flops, scratch=(), alias=()):
+    specs = [pl.BlockSpec(memory_space=pltpu.SMEM)]
+    for a in args[1:]:
+        if not isinstance(a, tuple):
+            specs.append(pl.BlockSpec(a.shape, lambda j: (0, 0)))
+        elif a[1] == 0:
+            specs.append(pl.BlockSpec((rows, a[0].shape[1]), lambda j: (j, 0)))
+        else:
+            specs.append(pl.BlockSpec((a[0].shape[0], rows), lambda j: (0, j)))
+    arrays = [a[0] if isinstance(a, tuple) else a for a in args]
     return pl.pallas_call(
-        update_kernel,
-        grid=(height // rows,),
-        in_specs=[
-            pl.BlockSpec(memory_space=pltpu.SMEM),
-            pl.BlockSpec((n, rows), lambda j: (0, j)),
-            *map(whole, (u, v, dest, own, sent)),
-            pl.BlockSpec((rows, w), lambda j: (j, 0)),
-        ],
-        out_specs=pl.BlockSpec((rows, w), lambda j: (j, 0)),
-        out_shape=jax.ShapeDtypeStruct(slab.shape, BF),
-        scratch_shapes=[pltpu.VMEM((2 * n, w + 128), BF)],
+        kernel,
+        grid=(out[0] // rows,),
+        in_specs=specs,
+        out_specs=pl.BlockSpec((rows, out[1]), lambda j: (j, 0)),
+        out_shape=jax.ShapeDtypeStruct(out, BF),
+        scratch_shapes=scratch,
+        input_output_aliases=dict(alias),
         compiler_params=ROOM,
-        cost_estimate=pl.CostEstimate(
-            flops=4 * height * n * w, bytes_accessed=2 * n * height + 4 * height * w, transcendentals=0
-        ),
-    )(row, panel, u, v, dest, own, sent, slab)
+        cost_estimate=pl.CostEstimate(flops=flops, bytes_accessed=6 * 2**20, transcendentals=0),
+    )(*arrays)
 
 
 def lines(first):
@@ -260,31 +264,33 @@
     home = jnp.where(row == 0, home, got)
     got = hand_on(home, 8)
     picked, place, dest, most = picks(jnp.int32(0))
-    near, got, picked = lax.optimization_barrier((near, got, picked))
+    near, picked = lax.optimization_barrier((near, picked))
+    panel = exchange(near, lines(1)).reshape(n, local_rows)
+    got, picked = lax.optimization_barrier((got, picked))
     home = jnp.where(row % 8 == 0, home, got)
     got = hand_on(home, 4)
-    panel = exchange(near, lines(1)).reshape(n, local_rows)
-    got, picked = lax.optimization_barrier((got, picked))
+    rows = lax.all_gather(picked, "prow", axis=0, tiled=True)
+    got, rows = lax.optimization_barrier((got, rows))
     home = jnp.where(row % 4 == 0, home, got)
     sent = hand_on(home, 2)
-    got = lax.all_gather(picked, "prow", axis=0, tiled=True)
-
-    def direct():
-        return solve(place_solve_kernel, r, parts, place, got)
-
-    def in_rounds():
+    u, v = solve(place_solve_kernel, r, parts, place, rows)
+
+    def in_rounds(_):
         def step(state):
             base, top = state
             picked, place, _, _ = picks(base)
-            got = lax.all_gather(picked, "prow", axis=0, tiled=True)
-            top = pl.pallas_call(add_kernel, out_shape=jax.ShapeDtypeStruct((n, w), BF))(top, place, got)
+            rows = lax.all_gather(picked, "prow", axis=0, tiled=True)
+            top = pl.pallas_call(add_kernel, out_shape=jax.ShapeDtypeStruct((n, w), BF))(top, place, rows)
             return base + CAP, top
 
         _, top = lax.while_loop(lambda s: s[0] < most[0], step, (jnp.int32(0), jnp.zeros((n, w), BF)))
-        return solve(solve_kernel, r, parts, top)
-
-    u, v = lax.cond(most[0] <= CAP, direct, in_rounds)
-    return update(r, panel, u, v, dest, home, sent, slab, 256)
+        return False, *solve(solve_kernel, r, parts, top)
+
+    _, u, v = lax.while_loop(lambda s: s[0], in_rounds, (most[0] > CAP, u, v))
+    flops = 2 * local_rows * n * w
+    scratch = [pltpu.VMEM((n, w + 128), BF)]
+    swapped = by_rows(swap_kernel, 256, slab.shape, (r, dest, home, sent, (slab, 0)), flops, scratch)
+    return by_rows(update_kernel, 256, slab.shape, (r, (panel, 1), u, v, (swapped, 0)), flops, alias=[(4, 0)])
 
 
 def solution(mesh):

time: 90.9 us -> 87.8 us (0.966)
  blocking collectives: 37.9 us -> 30.8 us
  Pallas kernels: 19.1 us -> 23.1 us
    all_gather x1, blocking collectives: 37.9 us -> 30.8 us  [step_of_panel(): rows = lax.all_gather(picked, 'prow', axis=0, tiled=True)]
    pallas_call x1 -> x2, Pallas kernels: 7.65 us -> 13.5 us  [by_rows(): pl.pallas_call(kernel, grid=(out[0] // rows,), in_specs=specs, out_specs=...]
    pallas_call x1, Pallas kernels: 4.04 us -> 2.41 us  [solve(): pl.pallas_call(kernel, in_specs=[pl.BlockSpec(memory_space=pltpu.SMEM)] +...]
  transfers between devices with their start and end apart: 6 -> 6, of which waited for: 1 -> 1; matrix products, arithmetic and copies ran while one was open for 2% -> 4% of each run, Pallas kernels for 13% -> 19%
where the time goes in v1:
time: 87.8 us; the launch traced here: 86.9 us
  blocking collectives  30.8 us (35%)
  starting transfers between devices  27.2 us (31%)
  Pallas kernels  23.1 us (26%)
  local copies, waits for them, and re-layouts  4.18 us (5%)
    all_gather x1, blocking collectives, step_of_panel(): rows = lax.all_gather(picked, 'prow', axis=0, tiled=True)  30.8 us
    all_to_all x2, starting transfers between devices, exchange(): lax.all_to_all(copies, ('prow', 'pcol'), 0, 0, axis_index_groups=groups)  23.7 us
    pallas_call x2, Pallas kernels, by_rows(): pl.pallas_call(kernel, grid=(out[0] // rows,), in_specs=specs, out_specs=...  13.5 us
    pallas_call x1, Pallas kernels, inverse(): pl.pallas_call(inverse_kernel, out_shape=[shape] * 2, scratch_shapes=[plt...  5.28 us
    ppermute x4, starting transfers between devices, hand_on(): lax.ppermute(home, 'prow', [(i, i + size // 2) for i in range(0, 16, size)])  3.48 us
    broadcast_in_dim x2, local copies, waits for them, and re-layouts, exchange(): copies = jnp.broadcast_to(block[None], (8,) + block.shape)  3.05 us
    pallas_call x1, Pallas kernels, solve(): pl.pallas_call(kernel, in_specs=[pl.BlockSpec(memory_space=pltpu.SMEM)] +...  2.41 us
    pallas_call x1, Pallas kernels, pick(): pl.pallas_call(pick_kernel, in_specs=[pl.BlockSpec(memory_space=pltpu.SME...  1.86 us
  transfers between devices with their start and end apart: 6, of which 1 were waited for; matrix products, arithmetic and copies ran while one was open for 4% of the time, Pallas kernels for 19%

profile of v1, /device:TPU:1, one launch (start us, length us, event | category | flops | bytes accessed | tf_op | source)
XLA Modules:
  0.0 86.9 jit_solution(16078058098925220105)
XLA Ops:
  0.0 0.0 copy-start.1
  0.0 1.1 %slice.3 = bf16[512,384]{1,0:T(8,128)(2,1)S(1)} slice(bf16[2048,384]{1,0:T(8,128)(2,1)} %slab_ref.3), slice={[0:512], [0:384]} | slice | bytes 786432 | tf_op jit(solution)/shard_map/slice | solution.py:260
  1.1 0.7 collective-permute-start
  1.8 1.5 %broadcast_in_dim.8 = bf16[8,8,2048]{2,1,0:T(8,128)(2,1)} broadcast(bf16[8,2048]{1,0:T(8,128)(2,1)} %param.11), dimensions={1,2} | broadcast | bytes 294912 | tf_op jit(solution)/shard_map/broadcast_in_dim | solution.py:241
  3.3 7.3 %all-to-all-start = ((bf16[8,8,2048]{2,1,0:T(8,128)(2,1)}), bf16[8,8,2048]{2,1,0:T(8,128)(2,1)S(1)}, u32[]{:S(2)}, u32[]{:S(2)}) async-start(bf16[8,8,2048]{2,1,0:T(8,128)(2,1)} %broadcast_in_dim.8), calls=%async_computation | async-start | bytes 524288 | tf_op jit(solution)/shard_map/all_to_all | solution.py:242
  10.6 0.0 copy-done.1
  10.6 0.0 copy-start.2
  10.6 0.0 copy-start.4
  10.6 5.3 %shard_map.47 = (bf16[512,512]{1,0:T(8,128)(2,1)}, bf16[512,512]{1,0:T(8,128)(2,1)}) custom-call(bf16[512,512]{1,0:T(8,128)(2,1)S(1)} %copy-done.1), custom_call_target="tpu_custom_call" | custom-call | flops 2000000000 | bytes 2097152 | tf_op jit(solution)/shard_map/pallas_call | solution.py:122
  15.9 0.0 collective-permute-done
  15.9 0.0 copy-done.2
  15.9 0.7 collective-permute-start.1
  16.7 0.1 pad_add_fusion.1.where_ref
  16.7 0.0 copy-done.4
  16.7 1.9 %shard_map.46 = (bf16[80,384]{1,0:T(8,128)(2,1)S(1)}, s32[512,1]{1,0:T(8,128)S(1)}, s32[1,512]{1,0:T(1,128)S(1)}, s32[1]{0:T(128)}) custom-call(s32[2]{0:T(128)S(1)} %pad_add_fusion.1.where_ref, s32[1,512]{1,0:T(1,128)S(1)} %bitcast.18, bf16[2048,384]{1,0:T(8,128)(2,1)S(1)} %copy-done.2), custom_call_target="tpu_custom_call" | custom-call | flops 2000000000 | bytes 1572864 | tf_op jit(solution)/shard_map/pallas_call | solution.py:60
  19.2 0.7 all-to-all-done
  19.9 1.6 %broadcast_in_dim.20 = bf16[8,64,2048]{2,1,0:T(8,128)(2,1)} broadcast(bf16[64,2048]{1,0:T(8,128)(2,1)S(1)} %bitcast.17), dimensions={1,2} | broadcast | bytes 2359296 | tf_op jit(solution)/shard_map/broadcast_in_dim | solution.py:241
  21.5 16.4 %all-to-all-start.1 = ((bf16[8,64,2048]{2,1,0:T(8,128)(2,1)}), bf16[8,64,2048]{2,1,0:T(8,128)(2,1)S(1)}, u32[]{:S(2)}, u32[]{:S(2)}) async-start(bf16[8,64,2048]{2,1,0:T(8,128)(2,1)} %broadcast_in_dim.20), calls=%async_computation.1 | async-start | bytes 4194304 | tf_op jit(solution)/shard_map/all_to_all | solution.py:242
  37.9 0.0 copy-start.5
  37.9 0.0 copy-start.7
  37.9 0.0 collective-permute-done.1
  37.9 0.1 broadcast_select_fusion.2
  38.0 0.8 collective-permute-start.2
  38.8 30.8 %all_gather.6.got_ref = bf16[1280,384]{1,0:T(8,128)(2,1)S(1)} all-gather(bf16[80,384]{1,0:T(8,128)(2,1)S(1)} %get-tuple-element.120), channel_id=1, replica_groups=mesh['prow'=16,'pcol'=64] {'prow'}, dimensions={0}, use_global_device_ids=true | all-gather | bytes 1044480 | tf_op jit(solution)/shard_map/all_gather | solution.py:272
  69.6 0.0 collective-permute-done.2
  69.7 1.3 %collective-permute-start.3 = (bf16[512,384]{1,0:T(8,128)(2,1)S(1)}, bf16[512,384]{1,0:T(8,128)(2,1)S(1)}, u32[]{:S(2)}, u32[]{:S(2)}) collective-permute-start(bf16[512,384]{1,0:T(8,128)(2,1)S(1)} %broadcast_select_fusion.own_ref), channel_id=1, source_target_pairs={{0,64},{128,192},{256,320},{384,448},{512,576},{640,704},{768,832}... | collective-permute-start | bytes 1179656 | tf_op jit(solution)/shard_map/ppermute | solution.py:246
  71.0 0.0 copy-done.5
  71.0 0.0 copy-done.7
  71.0 2.4 %shard_map.48 = (bf16[512,384]{1,0:T(8,128)(2,1)}, bf16[512,384]{1,0:T(8,128)(2,1)}) custom-call(s32[1]{0:T(128)} %bitcast.4.row_ref, bf16[512,512]{1,0:T(8,128)(2,1)S(1)} %copy-done.5, bf16[512,512]{1,0:T(8,128)(2,1)S(1)} %copy-done.7, s32[512,1]{1,0:T(8,128)S(1)} %get-tuple-element.116.place_ref, bf16[1280,384]{1,0:T(8,128)(2,1)S(1)} %all_gather.6.got_ref), custom_call_target="tpu_custom_call" | custom-call | flops 1000000000 | bytes 10000000 | tf_op jit(solution)/shard_map/pallas_call | solution.py:164
  73.4 0.0 collective-permute-done.3.sent_ref
  73.4 0.0 copy-start.3
  73.4 6.6 %shard_map.49.slab_ref = bf16[2048,384]{1,0:T(8,128)(2,1)} custom-call(s32[1]{0:T(128)} %bitcast.4.row_ref, s32[1,512]{1,0:T(1,128)S(1)} %get-tuple-element.126.dest_ref, bf16[512,384]{1,0:T(8,128)(2,1)S(1)} %broadcast_select_fusion.own_ref, bf16[512,384]{1,0:T(8,128)(2,1)S(1)} %collective-permute-done.3.sent_ref, bf16[2048,384]{1,0:T(8,128)(2,1)} %get-tuple-element.307), custom_call_target="tpu_custom_call" | custom-call | flops 805306368 | bytes 6291456 | tf_op jit(solution)/shard_map/pallas_call | solution.py:218
  80.0 0.0 all-to-all-done.1
  80.1 0.0 copy-done.3
  80.1 6.9 %shard_map.50 = bf16[2048,384]{1,0:T(8,128)(2,1)} custom-call(s32[1]{0:T(128)} %bitcast.4.row_ref, bf16[512,2048]{1,0:T(8,128)(2,1)S(1)} %bitcast.16, bf16[512,384]{1,0:T(8,128)(2,1)S(1)} %copy-done.3, bf16[512,384]{1,0:T(8,128)(2,1)} %get-tuple-element.303, bf16[2048,384]{1,0:T(8,128)(2,1)} %shard_map.49.slab_ref), custom_call_target="tpu_custom_call", output_to_operand_aliasing={{}: (4, {})} | custom-call | flops 805306368 | bytes 6291456 | tf_op jit(solution)/shard_map/pallas_call | solution.py:218
  (3 shorter events, 0.1 us)
Async XLA Ops:
  0.0 10.6 %copy-start.1 = (bf16[512,512]{1,0:T(8,128)(2,1)S(1)}, bf16[512,512]{1,0:T(8,128)(2,1)}, u32[]{:S(2)}) copy-start(bf16[512,512]{1,0:T(8,128)(2,1)} %l_ref.1) | copy-start | bytes 1572868
  1.1 14.8 %collective-permute-start = (bf16[512,384]{1,0:T(8,128)(2,1)S(1)}, bf16[512,384]{1,0:T(8,128)(2,1)S(1)}, u32[]{:S(2)}, u32[]{:S(2)}) collective-permute-start(bf16[512,384]{1,0:T(8,128)(2,1)S(1)} %slice.3), channel_id=1, source_target_pairs={{0,512},{1,513},{2,514},{3,515},{4,516},{5,517},{6,518},{7,519},{8... | collective-permute-start | bytes 1179656 | tf_op jit(solution)/shard_map/ppermute | solution.py:246
  3.3 16.6 %all-to-all-start = ((bf16[8,8,2048]{2,1,0:T(8,128)(2,1)}), bf16[8,8,2048]{2,1,0:T(8,128)(2,1)S(1)}, u32[]{:S(2)}, u32[]{:S(2)}) async-start(bf16[8,8,2048]{2,1,0:T(8,128)(2,1)} %broadcast_in_dim.8), calls=%async_computation | async-start | bytes 524288 | tf_op jit(solution)/shard_map/all_to_all | solution.py:242
  10.6 5.3 %copy-start.2 = (bf16[2048,384]{1,0:T(8,128)(2,1)S(1)}, bf16[2048,384]{1,0:T(8,128)(2,1)}, u32[]{:S(2)}) copy-start(bf16[2048,384]{1,0:T(8,128)(2,1)} %slab_ref.3) | copy-start | bytes 4718596
  10.6 6.1 %copy-start.4 = (s32[512]{0:T(512)S(1)}, s32[512]{0:T(512)}, u32[]{:S(2)}) copy-start(s32[512]{0:T(512)} %param.9) | copy-start | bytes 6148
  15.9 22.0 %collective-permute-start.1 = (bf16[512,384]{1,0:T(8,128)(2,1)S(1)}, bf16[512,384]{1,0:T(8,128)(2,1)S(1)}, u32[]{:S(2)}, u32[]{:S(2)}) collective-permute-start(bf16[512,384]{1,0:T(8,128)(2,1)S(1)} %broadcast_select_fusion.1), channel_id=1, source_target_pairs={{0,256},{512,768},{1,257},{513,769},{2,258},{514,770},{3,259},{515... | collective-permute-start | bytes 1179656 | tf_op jit(solution)/shard_map/ppermute | solution.py:246
  21.5 58.6 %all-to-all-start.1 = ((bf16[8,64,2048]{2,1,0:T(8,128)(2,1)}), bf16[8,64,2048]{2,1,0:T(8,128)(2,1)S(1)}, u32[]{:S(2)}, u32[]{:S(2)}) async-start(bf16[8,64,2048]{2,1,0:T(8,128)(2,1)} %broadcast_in_dim.20), calls=%async_computation.1 | async-start | bytes 4194304 | tf_op jit(solution)/shard_map/all_to_all | solution.py:242
  37.9 33.1 %copy-start.5 = (bf16[512,512]{1,0:T(8,128)(2,1)S(1)}, bf16[512,512]{1,0:T(8,128)(2,1)}, u32[]{:S(2)}) copy-start(bf16[512,512]{1,0:T(8,128)(2,1)} %get-tuple-element.241.a_ref) | copy-start | bytes 1572868
  37.9 33.1 %copy-start.7 = (bf16[512,512]{1,0:T(8,128)(2,1)S(1)}, bf16[512,512]{1,0:T(8,128)(2,1)}, u32[]{:S(2)}) copy-start(bf16[512,512]{1,0:T(8,128)(2,1)} %get-tuple-element.242.b_ref) | copy-start | bytes 1572868
  38.0 31.6 %collective-permute-start.2 = (bf16[512,384]{1,0:T(8,128)(2,1)S(1)}, bf16[512,384]{1,0:T(8,128)(2,1)S(1)}, u32[]{:S(2)}, u32[]{:S(2)}) collective-permute-start(bf16[512,384]{1,0:T(8,128)(2,1)S(1)} %broadcast_select_fusion.2), channel_id=1, source_target_pairs={{0,128},{256,384},{512,640},{768,896},{1,129},{257,385},{513,641},... | collective-permute-start | bytes 1179656 | tf_op jit(solution)/shard_map/ppermute | solution.py:246
  69.7 3.7 %collective-permute-start.3 = (bf16[512,384]{1,0:T(8,128)(2,1)S(1)}, bf16[512,384]{1,0:T(8,128)(2,1)S(1)}, u32[]{:S(2)}, u32[]{:S(2)}) collective-permute-start(bf16[512,384]{1,0:T(8,128)(2,1)S(1)} %broadcast_select_fusion.own_ref), channel_id=1, source_target_pairs={{0,64},{128,192},{256,320},{384,448},{512,576},{640,704},{768,832}... | collective-permute-start | bytes 1179656 | tf_op jit(solution)/shard_map/ppermute | solution.py:246
  73.4 6.6 %copy-start.3 = (bf16[512,384]{1,0:T(8,128)(2,1)S(1)}, bf16[512,384]{1,0:T(8,128)(2,1)}, u32[]{:S(2)}) copy-start(bf16[512,384]{1,0:T(8,128)(2,1)} %get-tuple-element.302) | copy-start | bytes 1179652
